TPU v7x, 32 devices: a whole 2x2x4 slice. The times are simulated.
32 devices in a mesh: cuts: 4 (over z), fsdp: 8 (over y, x, core).
Axes of the slice: x: 2, y: 2, z: 4, core: 2. Of those that a mesh axis runs over, the one named last changes fastest.
Arguments:
- tokens: bfloat16 [4096, 8192], P(('cuts', 'fsdp')), may hold values from -240 to 240
- norm_gain: bfloat16 [8192], P('fsdp'), may hold values from 0.5 to 1.5
- gate_weight: bfloat16 [8192, 256], P('fsdp'), may hold values from -0.0625 to 0.0625
- up_weight: bfloat16 [8192, 256], P('fsdp'), may hold values from -0.0625 to 0.0625
- down_weight: bfloat16 [256, 8192], P(None, 'fsdp'), may hold values from -0.375 to 0.375
- slice_grads: float32 [4, 3, 8192, 256], P('cuts', None, 'fsdp'), may hold values from -6 to 6
Outputs:
- branch_out: bfloat16 [4096, 8192], P(('cuts', 'fsdp'))
- grad_mean: float32 [3, 8192, 256], P(None, 'fsdp')
All inputs are finite; a program needn't handle non-finite values.
Results may differ from a plain program's by a relative error of at most 0.0065.
Values may be sent and summed in bfloat16 or wider, within the bound.
A program may use at most 64 MiB of HBM per device.

v0:
```python
import jax
import jax.numpy as jnp
from jax import lax
from jax.sharding import PartitionSpec as P


def average_grads(slice_grads):
    summed = lax.psum(slice_grads[0], "cuts")
    return summed / lax.axis_size("cuts")


def per_device(tokens, norm_gain, gate_weight, up_weight, down_weight, slice_grads):
    tok_float = tokens.astype(jnp.float32)
    inv_rms = lax.rsqrt(jnp.mean(tok_float * tok_float, axis=1, keepdims=True) + 1e-05)
    gathered = (
        lax.all_gather(gate_weight, "fsdp", axis=0, tiled=True),
        lax.all_gather(up_weight, "fsdp", axis=0, tiled=True),
        lax.all_gather(norm_gain, "fsdp", axis=0, tiled=True),
    )
    normed = (tok_float * inv_rms * gathered[2].astype(jnp.float32)[None, :]).astype(jnp.bfloat16)
    gate_out = jnp.dot(normed, gathered[0], preferred_element_type=jnp.float32)
    up_out = jnp.dot(normed, gathered[1], preferred_element_type=jnp.float32)
    hidden = (jax.nn.silu(gate_out) * up_out).astype(jnp.bfloat16)
    down_full = lax.all_gather(down_weight, "fsdp", axis=1, tiled=True)
    branch = jnp.dot(hidden, down_full, preferred_element_type=jnp.float32)
    grad_mean = average_grads(slice_grads)
    return (branch.astype(jnp.bfloat16), grad_mean)


def solution(mesh):
    return jax.shard_map(
        per_device,
        mesh=mesh,
        in_specs=(
            P(("cuts", "fsdp"), None),
            P("fsdp"),
            P("fsdp", None),
            P("fsdp", None),
            P(None, "fsdp"),
            P("cuts", None, "fsdp", None),
        ),
        out_specs=(P(("cuts", "fsdp"), None), P(None, "fsdp", None)),
        check_vma=False,
    )
```

profile of v0, /device:TPU:0, one launch (start us, length us, event | category | flops | bytes accessed | tf_op | source)
XLA Modules:
  0.0 156.7 jit_solution(2685609127519770182)
XLA Ops:
  8.0 0.0 copy-start.1
  8.0 0.0 copy-start
  8.0 0.0 all-reduce.2.cloned.1.call-start
  8.1 0.7 all-reduce.2.cloned.1.call-update
  8.8 0.0 all-gather.4.cloned.1.call-start
  8.8 0.5 all-gather.4.cloned.1.call-update
  9.3 0.0 all-gather.6.cloned.1.call-start
  9.4 0.5 all-gather.6.cloned.1.call-update
  9.9 0.0 all-gather.8.cloned.1.call-start
  10.0 0.5 all-gather.8.cloned.1.call-update
  10.5 0.0 copy-done.1
  10.5 10.4 %all_gather.12 = bf16[8192]{0:T(1024)(128)(2,1)S(1)} all-gather(bf16[1024]{0:T(1024)(128)(2,1)S(1)} %copy-done.1), channel_id=1, replica_groups=mesh['cuts'=4,'fsdp'=8] {'fsdp'}, dimensions={0}, use_global_device_ids=true | all-gather | bytes 18432 | tf_op jit(solution)/shard_map/all_gather | solution.py:18
  20.9 0.0 copy-done
  20.9 0.5 fusion
  21.4 113.6 %all-reduce.2.cloned.1.call-done = f32[3,1024,256]{2,1,0:T(8,128)} async-done(((f32[3,1024,256]{2,1,0:T(8,128)}), f32[3,1024,256]{2,1,0:T(8,128)}) %all-reduce.2.cloned.1.call-update) | async-done | bytes 3145744 | tf_op jit(solution)/shard_map/psum | solution.py:8
  135.0 3.8 %broadcast_multiply_fusion = f32[3,1024,256]{2,1,0:T(8,128)} fusion(f32[3,1024,256]{2,1,0:T(8,128)} %all-reduce.2.cloned.1.call-done), kind=kLoop, calls=%fused_computation.6 | loop fusion | flops 786432 | bytes 6291456 | tf_op jit(solution)/shard_map/div | solution.py:9
  138.8 0.0 all-gather.4.cloned.1.call-done
  138.8 2.9 %fusion.6 = f32[128,256]{1,0:T(8,128)S(1)} fusion(bf16[8192,256]{1,0:T(8,128)(2,1)} %all-gather.4.cloned.1.call-done, bf16[128,8192]{1,0:T(8,128)(2,1)S(1)} %copy-done, f32[8192]{0:T(1024)S(1)} %convert_element_type.16, f32[128]{0:T(128)S(1)} %add_rsqrt_fusion), kind=kOutput, calls=%fused_computation.9 | convolution fusion | flops 541065216 | bytes 6455808 | tf_op jit(solution)/shard_map/dot_general | solution.py:21
  141.8 0.0 all-gather.6.cloned.1.call-done
  141.8 0.0 all-gather.8.cloned.1.call-done
  141.8 7.2 %convolution_convert_fusion = bf16[128,8192]{1,0:T(8,128)(2,1)} fusion(bf16[256,8192]{1,0:T(8,128)(2,1)} %all-gather.8.cloned.1.call-done, bf16[8192,256]{1,0:T(8,128)(2,1)} %all-gather.6.cloned.1.call-done, bf16[128,8192]{1,0:T(8,128)(2,1)S(1)} %copy-done, f32[8192]{0:T(1024)S(1)} %convert_element_type.16, f32[128]{0:T(128)S(1)} %add_rsqrt_fusion, ...), kind=kOutput, calls=%fused_computation | convolution fusion | flops 1079181312 | bytes 12747264 | tf_op jit(solution)/shard_map/dot_general | solution.py:25
  (2 shorter events, 0.0 us)
Async XLA Ops:
  8.0 2.5 %copy-start.1 = (bf16[1024]{0:T(1024)(128)(2,1)S(1)}, bf16[1024]{0:T(1024)(128)(2,1)}, u32[]{:S(2)}) copy-start(bf16[1024]{0:T(1024)(128)(2,1)} %param.7) | copy-start | bytes 6148
  8.0 12.9 %copy-start = (bf16[128,8192]{1,0:T(8,128)(2,1)S(1)}, bf16[128,8192]{1,0:T(8,128)(2,1)}, u32[]{:S(2)}) copy-start(bf16[128,8192]{1,0:T(8,128)(2,1)} %param.6) | copy-start | bytes 6291460
  8.0 127.0 %all-reduce.2.cloned.1.call-start = ((), (), s32[]{:S(2)}) async-start(), calls=%async_computation.3 | async-start | bytes 6291456 | tf_op jit(solution)/shard_map/psum | solution.py:8
  8.8 130.1 %all-gather.4.cloned.1.call-start = ((), (), s32[]{:S(2)}) async-start(), calls=%async_computation | async-start | bytes 4718592 | tf_op jit(solution)/shard_map/all_gather | solution.py:16
  9.3 132.5 %all-gather.6.cloned.1.call-start = ((), (), s32[]{:S(2)}) async-start(), calls=%async_computation.1 | async-start | bytes 4718592 | tf_op jit(solution)/shard_map/all_gather | solution.py:17
  9.9 131.9 %all-gather.8.cloned.1.call-start = ((), (), s32[]{:S(2)}) async-start(), calls=%async_computation.2 | async-start | bytes 4718592 | tf_op jit(solution)/shard_map/all_gather | solution.py:24
Sparse Core Ops, SparseCore 0:
  11.2 123.7 all-reduce.1
Sparse Core Ops, SparseCore 1:
  11.1 39.2 all-gather.3
  52.1 36.4 all-gather.5
  90.4 36.4 all-gather.7
where the time goes:
time: 157 us
  waiting for transfers between devices  116 us (74%)
  between operations  15.7 us (10%)
  blocking collectives  10.4 us (7%)
  matrix products  10.2 us (6%)
  other arithmetic  4.32 us (3%)
    psum x1, waiting for transfers between devices, average_grads(): summed = lax.psum(slice_grads[0], 'cuts')  114 us
    all_gather x1, blocking collectives, per_device(): lax.all_gather(norm_gain, 'fsdp', axis=0, tiled=True)  10.4 us
    dot_general x1, matrix products, per_device(): branch = jnp.dot(hidden, down_full, preferred_element_type=jnp.float32)  7.24 us
    div x1, other arithmetic, average_grads(): return summed / lax.axis_size('cuts')  3.82 us
  transfers between devices with their start and end apart: 4, of which 1 were waited for; matrix products, arithmetic and copies ran while one was open for 5% of the time, Pallas kernels for 0%

commit v1 on v0

v1 whole, which is shorter than its diff:
```python
import functools

import jax
import jax.numpy as jnp
from jax import lax
from jax.experimental import pallas as pl
from jax.experimental.pallas import tpu as pltpu
from jax.sharding import PartitionSpec as P

MESH = pl.DeviceIdType.MESH
F32, BF16 = jnp.float32, jnp.bfloat16
CORES = 2
AHEAD = 2
ROW_PIECES = 8
K_BLOCKS = 2
GRAD_CHUNKS = 8
LANES = 128
ROWS = 16


def gray(pos, count):
    chip, bit = 0, 1
    while bit < count:
        chip = chip + bit * ((pos // bit + pos // (2 * bit)) % 2)
        bit *= 2
    return chip


def ungray(chip, count):
    pos, bit = 0, 1
    while bit < count:
        above, high = 0, bit
        while high < count:
            above = above + (chip // high) % 2
            high *= 2
        pos = pos + bit * (above % 2)
        bit *= 2
    return pos


def kernel(
    n, nc, tok_hbm, gain_ref, gate_hbm, up_hbm, down_hbm, grad_hbm, out_ref, mean_ref,
    wgu, wd, tok, gains, own_grad, rbuf, sbuf, tbuf, acc, hid, inv,
    load_sem, gain_send, gain_recv, link_send, pair_send, piece_recv,
    red_send, red_recv, tot_send, tot_recv,
):
    chips = n // CORES
    half_ring = chips // 2
    depth, width = gate_hbm.shape
    half = depth // 2
    row_piece = half // ROW_PIECES
    col_pieces = half // LANES
    pieces = ROW_PIECES + col_pieces
    k_block = half // K_BLOCKS

    me = lax.axis_index("fsdp")
    z = lax.axis_index("cuts")
    chip, core = me // CORES, me % CORES
    other = 1 - core
    partner = chip * CORES + other
    pos = ungray(chip, chips)

    def device(offset, which):
        return gray((pos + offset + chips) % chips, chips) * CORES + which

    right, left = device(1, core), device(-1, core)

    loads = [
        pltpu.make_async_copy(gate_hbm, wgu.at[me, :, pl.ds(0, width)], load_sem.at[0]),
        pltpu.make_async_copy(up_hbm, wgu.at[me, :, pl.ds(width, width)], load_sem.at[1]),
        pltpu.make_async_copy(down_hbm, wd.at[me], load_sem.at[2]),
        pltpu.make_async_copy(grad_hbm, own_grad, load_sem.at[3]),
        pltpu.make_async_copy(tok_hbm, tok, load_sem.at[4]),
    ]
    for load in loads:
        load.start()
    gains[me] = gain_ref[...].astype(F32)

    barrier = pltpu.get_barrier_semaphore()
    for step in range(1, n):
        pl.semaphore_signal(barrier, inc=1, device_id={"fsdp": (me + step) % n}, device_id_type=MESH)

    for step in (1, nc - 1):
        pl.semaphore_signal(barrier, inc=1, device_id={"cuts": (z + step) % nc}, device_id_type=MESH)
    pl.semaphore_wait(barrier, n + 1)

    def remote(src, dst, send, recv, to):
        return pltpu.make_async_remote_copy(
            src_ref=src, dst_ref=dst, send_sem=send, recv_sem=recv, device_id=to, device_id_type=MESH
        )

    def piece(origin, h, i):
        if i < ROW_PIECES:
            return wgu.at[origin, pl.ds(h * half + i * row_piece, row_piece), :]
        return wd.at[origin, :, pl.ds(h * half + (i - ROW_PIECES) * LANES, LANES)]

    def move(origin, h, i, send, to):
        ref = piece(origin, h, i)
        return remote(ref, ref, send, piece_recv.at[origin, h, i], {"fsdp": to})

    def halves(way, distance):
        both = (0, 1) if way == 0 else (1, 0)
        return both if distance < half_ring else both[:1]

    sent = []

    def link(way, distance, origin, h, i):
        copy = move(origin, h, i, link_send.at[way, distance - 1, h, i], right if way == 0 else left)
        copy.start()
        sent.append(copy)

    def pair(chip_offset, origin, h, i):
        copy = move(origin, h, i, pair_send.at[chip_offset % chips, h, i], partner)
        copy.start()
        sent.append(copy)

    def send_own(i):
        for turn in range(2):
            for way in range(2):
                order = halves(way, 1)
                if turn < len(order):
                    link(way, 1, me, order[turn], i)
        for h in range(2):
            pair(0, me, h, i)

    loads[0].wait()
    loads[1].wait()
    for i in range(AHEAD):
        send_own(i)
    gain_copies = []
    for step in range(1, n):
        copy = remote(
            gains.at[me], gains.at[me], gain_send.at[step], gain_recv.at[step], {"fsdp": (me + step) % n}
        )
        copy.start()
        gain_copies.append(copy)
    loads[2].wait()
    loads[3].wait()

    rows = own_grad.shape[0] // (2 * GRAD_CHUNKS)
    roots = ((nc - 1) // 2, nc // 2)

    def grad_tick(t):
        for g, root in enumerate(roots):
            deepest = max(root, nc - 1 - root)
            on_left = z < root
            side = jnp.where(on_left, 0, 1)
            inner = jnp.where(on_left, z + 1, z - 1)
            outer = jnp.where(on_left, z - 1, z + 1)
            outermost = jnp.where(on_left, z == 0, z == nc - 1)

            def span(j):
                return pl.ds(pl.multiple_of((g * GRAD_CHUNKS + j) * rows, rows), rows)

            def red(j, s, to):
                return remote(
                    sbuf.at[span(j), :], rbuf.at[s, span(j), :],
                    red_send.at[g, j], red_recv.at[s, g, j], {"cuts": to},
                )

            def tot(j, s, to):
                return remote(
                    tbuf.at[span(j), :], tbuf.at[span(j), :], tot_send.at[s, g, j], tot_recv.at[g, j], {"cuts": to}
                )

            j = t - jnp.where(on_left, z, nc - 1 - z)

            @pl.when((z != root) & (j >= 0) & (j < GRAD_CHUNKS))
            def _():
                @pl.when(outermost)
                def _():
                    sbuf[span(j), :] = own_grad[span(j), :].astype(BF16)

                @pl.when(jnp.logical_not(outermost))
                def _():
                    red(j, side, inner).wait_recv()
                    sbuf[span(j), :] = (own_grad[span(j), :] + rbuf[side, span(j), :].astype(F32)).astype(BF16)

                red(j, side, inner).start()

            jm = t - deepest
            if 0 <= jm < GRAD_CHUNKS:

                @pl.when(z == root)
                def _():
                    total = own_grad[span(jm), :]
                    if root > 0:
                        red(jm, 0, z - 1).wait_recv()
                        total = total + rbuf[0, span(jm), :].astype(F32)
                    if root < nc - 1:
                        red(jm, 1, z + 1).wait_recv()
                        total = total + rbuf[1, span(jm), :].astype(F32)
                    mean = (total / nc).astype(BF16)
                    tbuf[span(jm), :] = mean
                    mean_ref[span(jm), :] = mean.astype(F32)
                    if root > 0:
                        tot(jm, 0, z - 1).start()
                    if root < nc - 1:
                        tot(jm, 1, z + 1).start()

            jb = t - deepest - jnp.where(on_left, root - z, z - root)

            @pl.when((z != root) & (jb >= 0) & (jb < GRAD_CHUNKS))
            def _():
                tot(jb, side, inner).wait_recv()

                @pl.when(jnp.logical_not(outermost))
                def _():
                    tot(jb, side, outer).start()

                mean_ref[span(jb), :] = tbuf[span(jb), :].astype(F32)

    def grad_end():
        for g, root in enumerate(roots):
            for j in range(GRAD_CHUNKS):
                at = pl.ds((g * GRAD_CHUNKS + j) * rows, rows)
                on_left = z < root
                side = jnp.where(on_left, 0, 1)
                outermost = jnp.where(on_left, z == 0, z == nc - 1)

                def wait(sem, to):
                    remote(sbuf.at[at, :], tbuf.at[at, :], sem, tot_recv.at[g, j], {"cuts": to}).wait_send()

                @pl.when(z != root)
                def _():
                    wait(red_send.at[g, j], jnp.where(on_left, z + 1, z - 1))

                    @pl.when(jnp.logical_not(outermost))
                    def _():
                        wait(tot_send.at[side, g, j], jnp.where(on_left, z - 1, z + 1))

                @pl.when(z == root)
                def _():
                    if root > 0:
                        wait(tot_send.at[0, g, j], z - 1)
                    if root < nc - 1:
                        wait(tot_send.at[1, g, j], z + 1)

    def ring_tick(t):
        if AHEAD <= t + AHEAD < pieces:
            send_own(t + AHEAD)
        for distance in range(1, half_ring + 1):
            i = t - (distance - 1)
            if not 0 <= i < pieces:
                continue
            for turn in range(2):
                for way in range(2):
                    order = halves(way, distance)
                    if turn >= len(order):
                        continue
                    h = order[turn]
                    offset = -distance if way == 0 else distance
                    origin = device(offset, core)
                    move(origin, h, i, link_send.at[way, 0, h, i], right).wait_recv()
                    if distance < half_ring and h in halves(way, distance + 1):
                        link(way, distance + 1, origin, h, i)
                    pair(offset, origin, h, i)

    def wait_partner(lo, hi):
        def one(c, _):
            origin = c * CORES + other
            for i in range(lo, hi):
                for h in range(2):
                    move(origin, h, i, pair_send.at[0, h, i], partner).wait_recv()
            return 0

        lax.fori_loop(0, chips, one, 0)

    def gate_up(which, b):
        def one(c, _):
            origin = c * CORES + which
            for h in range(2):
                first = h * half + b * k_block
                at = pl.ds(pl.multiple_of(origin * depth + first, LANES), k_block)
                scaled = tok[:, at].astype(F32) * inv[...] * gains[origin, :, pl.ds(first, k_block)]
                acc[...] += jnp.dot(
                    scaled.astype(BF16), wgu[origin, pl.ds(first, k_block), :], preferred_element_type=F32
                )
            return 0

        lax.fori_loop(0, chips, one, 0)

    def down(which, i):
        def one(c, _):
            origin = c * CORES + which
            for h in range(2):
                first = h * half + (i - ROW_PIECES) * LANES
                at = pl.ds(pl.multiple_of(origin * depth + first, LANES), LANES)
                out_ref[:, at] = jnp.dot(
                    hid[...], wd[origin, :, pl.ds(first, LANES)], preferred_element_type=F32
                ).astype(BF16)
            return 0

        lax.fori_loop(0, chips, one, 0)

    def norms():
        loads[4].wait()
        total = jnp.zeros((tok.shape[0], 1), F32)

        def one(c, total):
            part = tok[:, pl.ds(pl.multiple_of(c * depth, LANES), depth)].astype(F32)
            return total + jnp.sum(part * part, axis=1, keepdims=True)

        total = lax.fori_loop(0, n, one, total)
        inv[...] = lax.rsqrt(total / tok.shape[1] + 1e-05)
        acc[...] = jnp.zeros_like(acc)

    def finish_hidden():
        gate, up = acc[:, :width], acc[:, width:]
        hid[...] = (gate / (1.0 + jnp.exp(-gate)) * up).astype(BF16)

    work = {}

    def at_tick(t, job):
        work.setdefault(t, []).append(job)

    at_tick(0, norms)
    ready = 0
    for b in range(K_BLOCKS):
        lo, hi = b * ROW_PIECES // K_BLOCKS, (b + 1) * ROW_PIECES // K_BLOCKS
        own_tick, pair_tick = hi - 1 + half_ring - 1, hi - 1 + half_ring
        if b == 0:

            def gains_here():
                for copy in gain_copies:
                    copy.wait_recv()

            at_tick(own_tick, gains_here)
        at_tick(own_tick, functools.partial(gate_up, core, b))
        at_tick(pair_tick, functools.partial(wait_partner, lo, hi))
        at_tick(pair_tick, functools.partial(gate_up, other, b))
        ready = pair_tick
    at_tick(ready, finish_hidden)
    for i in range(ROW_PIECES, pieces):
        at_tick(max(ready + 1, i + half_ring - 1), functools.partial(down, core, i))
        pair_tick = max(ready + 1, i + half_ring)
        at_tick(pair_tick, functools.partial(wait_partner, i, i + 1))
        at_tick(pair_tick, functools.partial(down, other, i))
    farthest = max(max(r, nc - 1 - r) for r in roots)
    ticks = max(max(work) + 1, GRAD_CHUNKS + 2 * farthest)
    for t in range(ticks):
        ring_tick(t)
        grad_tick(t)
        for job in work.get(t, ()):
            job()

    for copy in sent + gain_copies:
        copy.wait_send()
    grad_end()


def fits(n, nc, depth, width, grad_rows):
    chips = n // CORES
    ring = n % CORES == 0 and chips >= 2 and chips & (chips - 1) == 0
    whole = depth % (2 * LANES * K_BLOCKS) == 0 and depth % (2 * ROW_PIECES * ROWS) == 0
    return ring and nc > 1 and whole and width % LANES == 0 and grad_rows % (2 * GRAD_CHUNKS * ROWS) == 0


def plain(tokens, norm_gain, gate_weight, up_weight, down_weight, slice_grads):
    tok = tokens.astype(F32)
    inv = lax.rsqrt(jnp.mean(tok * tok, axis=1, keepdims=True) + 1e-05)
    gate_full, up_full, gain = (
        lax.all_gather(part, "fsdp", axis=0, tiled=True) for part in (gate_weight, up_weight, norm_gain)
    )
    normed = (tok * inv * gain.astype(F32)[None, :]).astype(BF16)
    gate = jnp.dot(normed, gate_full, preferred_element_type=F32)
    up = jnp.dot(normed, up_full, preferred_element_type=F32)
    hidden = (jax.nn.silu(gate) * up).astype(BF16)
    down_full = lax.all_gather(down_weight, "fsdp", axis=1, tiled=True)
    branch = jnp.dot(hidden, down_full, preferred_element_type=F32).astype(BF16)
    return branch, lax.psum(slice_grads[0], "cuts") / lax.axis_size("cuts")


def solution(mesh):
    n, nc = mesh.shape["fsdp"], mesh.shape["cuts"]

    def per_device(tokens, norm_gain, gate_weight, up_weight, down_weight, slice_grads):
        depth, width = gate_weight.shape
        grads = slice_grads.reshape(-1, slice_grads.shape[-1])
        if not fits(n, nc, depth, width, grads.shape[0]):
            return plain(tokens, norm_gain, gate_weight, up_weight, down_weight, slice_grads)
        chips = n // CORES
        pieces = ROW_PIECES + depth // 2 // LANES
        hbm, vmem = pl.BlockSpec(memory_space=pl.ANY), pl.BlockSpec(memory_space=pltpu.VMEM)
        dma = pltpu.SemaphoreType.DMA
        branch, mean = pl.pallas_call(
            functools.partial(kernel, n, nc),
            out_shape=(
                jax.ShapeDtypeStruct(tokens.shape, BF16),
                jax.ShapeDtypeStruct(grads.shape, F32),
            ),
            in_specs=[hbm, vmem, hbm, hbm, hbm, hbm],
            out_specs=(vmem, vmem),
            scratch_shapes=[
                pltpu.VMEM((n, depth, 2 * width), BF16),
                pltpu.VMEM((n, width, depth), BF16),
                pltpu.VMEM(tokens.shape, BF16),
                pltpu.VMEM((n, 1, depth), F32),
                pltpu.VMEM(grads.shape, F32),
                pltpu.VMEM((2,) + grads.shape, BF16),
                pltpu.VMEM(grads.shape, BF16),
                pltpu.VMEM(grads.shape, BF16),
                pltpu.VMEM((tokens.shape[0], 2 * width), F32),
                pltpu.VMEM((tokens.shape[0], width), BF16),
                pltpu.VMEM((tokens.shape[0], 1), F32),
                dma((5,)),
                dma((n,)),
                dma((n,)),
                dma((2, chips // 2, 2, pieces)),
                dma((chips, 2, pieces)),
                dma((n, 2, pieces)),
                dma((2, GRAD_CHUNKS)),
                dma((2, 2, GRAD_CHUNKS)),
                dma((2, 2, GRAD_CHUNKS)),
                dma((2, GRAD_CHUNKS)),
            ],
            compiler_params=pltpu.CompilerParams(collective_id=0, has_side_effects=True),
        )(tokens, norm_gain.reshape(1, -1), gate_weight, up_weight, down_weight, grads)
        return branch, mean.reshape(slice_grads.shape[1:])

    return jax.shard_map(
        per_device,
        mesh=mesh,
        in_specs=(
            P(("cuts", "fsdp"), None),
            P("fsdp"),
            P("fsdp", None),
            P("fsdp", None),
            P(None, "fsdp"),
            P("cuts", None, "fsdp", None),
        ),
        out_specs=(P(("cuts", "fsdp"), None), P(None, "fsdp", None)),
        check_vma=False,
    )
```

time: 157 us -> 82 us (0.52)
  waiting for transfers between devices: 116 us -> 0 us
  Pallas kernels: 0 us -> 75 us
  between operations: 15.7 us -> 0.65 us
  blocking collectives: 10.4 us -> 0 us
  matrix products: 10.2 us -> 0 us
  local copies, waits for them, and re-layouts: 0.01 us -> 6.19 us
  other arithmetic: 4.32 us -> 0 us
    psum x1 -> x0, waiting for transfers between devices: 114 us -> none  [average_grads(): summed = lax.psum(slice_grads[0], 'cuts')]
    pallas_call x0 -> x1, Pallas kernels: none -> 75 us  [per_device(): pl.pallas_call(functools.partial(kernel, n, nc), out_shape=(jax.ShapeDtyp...]
    all_gather x1 -> x0, blocking collectives: 10.4 us -> none  [per_device(): lax.all_gather(norm_gain, 'fsdp', axis=0, tiled=True)]
    dot_general x2 -> x0, matrix products: 10.2 us -> none  [the longest x1 7.24 us: per_device(): branch = jnp.dot(hidden, down_full, preferred_element_type=jnp.float32)]
    unnamed x4, local copies, waits for them, and re-layouts: 0.01 us -> 4.91 us
    div x1 -> x0, other arithmetic: 3.82 us -> none  [average_grads(): return summed / lax.axis_size('cuts')]
    unnamed x4 -> x0, waiting for transfers between devices: 2.26 us -> none
  transfers between devices with their start and end apart: 4 -> 0, of which waited for: 1 -> 0; matrix products, arithmetic and copies ran while one was open for 5% -> 0% of each run, Pallas kernels for 0% -> 0%
where the time goes in v1:
time: 82 us; the launch traced here: 81.8 us
  Pallas kernels  75 us (91%)
  local copies, waits for them, and re-layouts  6.19 us (8%)
    pallas_call x1, Pallas kernels, per_device(): pl.pallas_call(functools.partial(kernel, n, nc), out_shape=(jax.ShapeDtyp...  75 us
    unnamed x4, local copies, waits for them, and re-layouts  4.91 us

profile of v1, /device:TPU:0, one launch (start us, length us, event | category | flops | bytes accessed | tf_op | source)
XLA Modules:
  0.0 81.8 jit_solution(9173837757618901546)
XLA Ops:
  0.6 1.3 %reshape.13.gain_ref = bf16[1,1024]{1,0:T(2,128)(2,1)} reshape(bf16[1024]{0:T(1024)(128)(2,1)} %param.7) | data formatting | bytes 4096 | tf_op jit(solution)/shard_map/reshape | solution.py:418
  1.9 75.0 %shard_map.77 = (bf16[128,8192]{1,0:T(8,128)(2,1)}, f32[3072,256]{1,0:T(8,128)}) custom-call(bf16[128,8192]{1,0:T(8,128)(2,1)} %tok_hbm.1, bf16[1,1024]{1,0:T(2,128)(2,1)} %reshape.13.gain_ref, bf16[1024,256]{1,0:T(8,128)(2,1)} %gate_hbm.1, bf16[1024,256]{1,0:T(8,128)(2,1)} %up_hbm.1, bf16[256,1024]{1,0:T(8,128)(2,1)} %down_hbm.1, f32[3072,256]{1,0:T(8,128)} %bitcast.2), custom_call_target="tpu_custom_call" | custom-call | tf_op jit(solution)/shard_map/pallas_call | solution.py:386
  76.9 0.0 copy-start
  76.9 3.2 %copy.10 = bf16[128,8192]{1,0:T(8,128)(2,1)} copy(bf16[128,8192]{1,0:T(8,128)(2,1)} %get-tuple-element.8) | data formatting | bytes 4194304
  80.2 0.0 copy-done
  80.2 1.7 %copy.11 = f32[3,1024,256]{2,1,0:T(8,128)} copy(f32[3,1024,256]{2,1,0:T(8,128)S(1)} %bitcast.3) | data formatting | bytes 6291456
Async XLA Ops:
  76.9 3.3 %copy-start = (f32[3072,256]{1,0:T(8,128)S(1)}, f32[3072,256]{1,0:T(8,128)}, u32[]{:S(2)}) copy-start(f32[3072,256]{1,0:T(8,128)} %get-tuple-element.5) | copy-start | bytes 9437188
